TPU v7x, 512 devices: a whole 4x4x16 slice. The times are simulated.
512 devices in a mesh: feat: 64 (over y, z), samp: 8 (over x, core).
Axes of the slice: x: 4, y: 4, z: 16, core: 2. Of those that a mesh axis runs over, the one named last changes fastest.
Arguments:
- features: bfloat16 [1024, 524288], P('samp', 'feat'), may hold values from -14 to 14
- labels: int32 [1024, 32], P('samp'), may hold values from -1 to 1, as said below
- alpha_start: float32 [1024, 32], P('samp'), may hold values from 0 to 1
- order: int32 [2, 1024], P(None, 'samp'), may hold values from 0 to 127, as said below
Outputs:
- alpha: float32 [1024, 32], P('samp')
- scores: float32 [1024, 32], P('samp')
Inputs may be any that keep to these rules, and one draw needn't show every extreme that they name: `labels`: every entry is -1 or +1. `order`: for each round, each aligned block of 128 entries (one partition) is a permutation of 0 to 127.
All inputs are finite; a program needn't handle non-finite values.
Results may differ from a plain program's by a relative error of at most 0.004.
Values may be sent and summed in bfloat16 or wider, within the bound.
A program may use at most 64 MiB of HBM per device.

v0:
```python
import functools

import jax
import jax.numpy as jnp
from jax import lax
from jax.sharding import Mesh
from jax.sharding import PartitionSpec as P

BLOCK = 64
ROUNDS = 2
FEAT = ("feat_0", "feat_1")


reg_scale = 0.9


def from_everyone(x, axis):
    size = lax.axis_size(axis)
    return lax.all_to_all(jnp.broadcast_to(x[None], (size, *x.shape)), axis, 0, 0, tiled=True)


def of_everyone(x, axis):
    return from_everyone(x, axis).astype(jnp.float32).sum(axis=0)


def over_axes(x, axes):
    return functools.reduce(lax.psum, axes, x)


def of_everyone_2(x, axis):
    everything = from_everyone(x, axis)
    return jnp.sum(everything, axis=0)


def contract_rows(left_side, right_side):
    return lax.dot_general(
        left_side, right_side, (((0,), (0,)), ((), ())), preferred_element_type=jnp.float32
    )


def contract_cols(left_side, right_side):
    return lax.dot_general(
        left_side, right_side, (((1,), (1,)), ((), ())), preferred_element_type=jnp.float32
    )


def dual_update(before, margins, block_signs, block_norms, lam_total):
    return jnp.clip(
        before + lam_total * (1.0 - block_signs * margins) / block_norms[:, None], 0.0, 1.0
    )


def per_device(features, labels, alpha_start, order):
    row_count = features.shape[0]
    block_total = row_count // BLOCK
    part_count = lax.axis_size("samp")
    lam_total = reg_scale * features.shape[1] * lax.axis_size(FEAT)
    signs_all = labels.astype(jnp.float32)
    coeffs = (alpha_start * signs_all).astype(jnp.bfloat16)
    piece = (contract_rows(coeffs, features) / lam_total).astype(jnp.bfloat16)
    weights = of_everyone(piece, "samp").astype(jnp.float32)
    norms_all = (
        over_axes(
            jnp.einsum("rf,rf->r", features, features, preferred_element_type=jnp.float32), FEAT
        )
        + 1.0
    )
    alpha_now = alpha_start
    for round_num in range(ROUNDS):
        row_order = order[round_num]

        def feature_block(block_num, carry, row_order=row_order):
            local_weights, local_alpha = carry
            chosen = lax.dynamic_slice_in_dim(row_order, block_num * BLOCK, BLOCK)
            picked = jnp.take(features, chosen, axis=0)
            margins = of_everyone_2(contract_cols(picked, local_weights.astype(jnp.bfloat16)), FEAT)
            before = jnp.take(local_alpha, chosen, axis=0)
            block_signs = jnp.take(signs_all, chosen, axis=0)
            updated = dual_update(
                before, margins, block_signs, jnp.take(norms_all, chosen, axis=0), lam_total
            )
            change = ((updated - before) * block_signs).astype(jnp.bfloat16)
            return (
                local_weights + contract_rows(change, picked) / lam_total,
                local_alpha.at[chosen].set(updated),
            )

        local_weights, local_alpha = lax.fori_loop(
            0, block_total, feature_block, (weights, alpha_now)
        )
        delta_weights = (local_weights - weights).astype(jnp.bfloat16)
        summed = of_everyone(delta_weights, "samp").astype(jnp.float32)
        weights = weights + summed / part_count
        alpha_now = alpha_now + (local_alpha - alpha_now) / part_count
    scores = over_axes(contract_cols(features, weights.astype(jnp.bfloat16)), FEAT)
    return (alpha_now, scores)


def solution(mesh):
    finer = Mesh(mesh.devices.reshape(4, 16, mesh.shape["samp"]), ("feat_0", "feat_1", "samp"))
    placed = (P("samp", FEAT), P("samp", None), P("samp", None), P(None, "samp"))
    return jax.shard_map(
        per_device,
        mesh=finer,
        in_specs=placed,
        out_specs=(P("samp", None), P("samp", None)),
        check_vma=False,
    )
```

profile of v0, /device:TPU:2, one launch (start us, length us, event | category | flops | bytes accessed | tf_op | source)
XLA Modules:
  0.0 499.9 jit_solution(18110227024276414921)
XLA Ops:
  2.3 2.0 fusion.18
  4.3 2.5 broadcast_in_dim.94
  6.8 10.4 %all-to-all-start.2 = ((bf16[8,32,8192]{2,1,0:T(8,128)(2,1)}), bf16[8,32,8192]{2,1,0:T(8,128)(2,1)}, u32[]{:S(2)}, u32[]{:S(2)}) async-start(bf16[8,32,8192]{2,1,0:T(8,128)(2,1)} %broadcast_in_dim.94), calls=%async_computation.2 | async-start | bytes 8388608 | tf_op jit(solution)/shard_map/all_to_all | solution.py:19
  17.7 7.7 %psum.28 = f32[128]{0:T(128)S(1)} all-reduce(f32[128]{0:T(128)S(1)} %fusion.19), channel_id=1, replica_groups=mesh['feat_0'=4,'feat_1'=16,'samp'=8] {'feat_0'}, use_global_device_ids=true, to_apply=%region_1.0 | all-reduce | flops 128 | bytes 1024 | tf_op jit(solution)/shard_map/psum | solution.py:27
  25.4 34.1 %psum.29 = f32[128]{0:T(128)S(1)} all-reduce(f32[128]{0:T(128)S(1)} %psum.28), channel_id=1, replica_groups=mesh['feat_0'=4,'feat_1'=16,'samp'=8] {'feat_1'}, use_global_device_ids=true, to_apply=%region_2.0 | all-reduce | flops 128 | bytes 1024 | tf_op jit(solution)/shard_map/psum | solution.py:27
  59.6 5.9 %all-to-all-done.2 = bf16[8,32,8192]{2,1,0:T(8,128)(2,1)} async-done(((bf16[8,32,8192]{2,1,0:T(8,128)(2,1)}), bf16[8,32,8192]{2,1,0:T(8,128)(2,1)}, u32[]{:S(2)}, u32[]{:S(2)}) %all-to-all-start.2) | async-done | bytes 4194336 | tf_op jit(solution)/shard_map/all_to_all | solution.py:19
  65.5 2.9 convert_reduce_fusion.2
  70.5 120.0 %while.30 = (s32[]{:T(128)}, f32[32,8192]{1,0:T(8,128)}, f32[128,32]{1,0:T(8,128)S(1)}, s32[128]{0:T(128)S(1)}, f32[128,32]{1,0:T(8,128)S(1)}, /*index=5*/bf16[1...) while((s32[]{:T(128)}, f32[32,8192]{1,0:T(8,128)}, ...), condition=%wide.region_6.10_spmd, body=%wide.region_3.9_spmd.sunk | while | flops 69113472 | bytes 13329043 | solution.py:88
  71.8 1.7 fusion.32
  74.7 2.7 reshape.176
  77.3 13.7 %all-to-all-start = ((f32[64,1,2048]{2,1,0:T(1,128)}), f32[64,1,2048]{2,1,0:T(1,128)}, u32[]{:S(2)}, u32[]{:S(2)}) async-start(f32[64,1,2048]{2,1,0:T(1,128)} %reshape.176), calls=%async_computation | async-start | bytes 1048576 | tf_op jit(solution)/shard_map/while/body/eval_jaxpr/all_to_all | solution.py:19
  93.0 29.3 %all-to-all-done = f32[64,1,2048]{2,1,0:T(1,128)} async-done(((f32[64,1,2048]{2,1,0:T(1,128)}), f32[64,1,2048]{2,1,0:T(1,128)}, u32[]{:S(2)}, u32[]{:S(2)}) %all-to-all-start) | async-done | bytes 524320 | tf_op jit(solution)/shard_map/while/body/eval_jaxpr/all_to_all | solution.py:19
  122.8 3.7 reduce.6
  126.5 2.5 reshape.177
  130.4 2.7 fusion.33
  135.2 1.7 fusion.32
  138.1 2.7 reshape.176
  140.7 6.9 %all-to-all-start = ((f32[64,1,2048]{2,1,0:T(1,128)}), f32[64,1,2048]{2,1,0:T(1,128)}, u32[]{:S(2)}, u32[]{:S(2)}) async-start(f32[64,1,2048]{2,1,0:T(1,128)} %reshape.176), calls=%async_computation | async-start | bytes 1048576 | tf_op jit(solution)/shard_map/while/body/eval_jaxpr/all_to_all | solution.py:19
  149.6 29.2 %all-to-all-done = f32[64,1,2048]{2,1,0:T(1,128)} async-done(((f32[64,1,2048]{2,1,0:T(1,128)}), f32[64,1,2048]{2,1,0:T(1,128)}, u32[]{:S(2)}, u32[]{:S(2)}) %all-to-all-start) | async-done | bytes 524320 | tf_op jit(solution)/shard_map/while/body/eval_jaxpr/all_to_all | solution.py:19
  179.3 3.7 reduce.6
  183.1 2.5 reshape.177
  186.9 2.7 fusion.33
  190.5 1.6 subtract_convert_fusion.1
  192.1 2.5 broadcast_in_dim.95
  194.6 6.0 %all-to-all-start.3 = ((bf16[8,32,8192]{2,1,0:T(8,128)(2,1)}), bf16[8,32,8192]{2,1,0:T(8,128)(2,1)}, u32[]{:S(2)}, u32[]{:S(2)}) async-start(bf16[8,32,8192]{2,1,0:T(8,128)(2,1)} %broadcast_in_dim.95), calls=%async_computation.3 | async-start | bytes 8388608 | tf_op jit(solution)/shard_map/all_to_all | solution.py:19
  200.8 48.1 %all-to-all-done.3 = bf16[8,32,8192]{2,1,0:T(8,128)(2,1)} async-done(((bf16[8,32,8192]{2,1,0:T(8,128)(2,1)}), bf16[8,32,8192]{2,1,0:T(8,128)(2,1)}, u32[]{:S(2)}, u32[]{:S(2)}) %all-to-all-start.3) | async-done | bytes 4194336 | tf_op jit(solution)/shard_map/all_to_all | solution.py:19
  248.9 2.9 convert_reduce_fusion.1
  254.1 113.2 %while.31 = (s32[]{:T(128)}, f32[32,8192]{1,0:T(8,128)}, f32[128,32]{1,0:T(8,128)S(1)}, s32[128]{0:T(128)S(1)}, f32[128,32]{1,0:T(8,128)S(1)}, /*index=5*/bf16[1...) while((s32[]{:T(128)}, f32[32,8192]{1,0:T(8,128)}, ...), condition=%wide.region_11.15_spmd, body=%wide.region_8.14_spmd.sunk | while | flops 69113472 | bytes 13329043 | solution.py:88
  255.4 1.7 fusion.35
  258.2 2.7 reshape.188
  260.9 6.9 %all-to-all-start.1 = ((f32[64,1,2048]{2,1,0:T(1,128)}), f32[64,1,2048]{2,1,0:T(1,128)}, u32[]{:S(2)}, u32[]{:S(2)}) async-start(f32[64,1,2048]{2,1,0:T(1,128)} %reshape.188), calls=%async_computation.1 | async-start | bytes 1048576 | tf_op jit(solution)/shard_map/while/body/eval_jaxpr/all_to_all | solution.py:19
  269.8 29.3 %all-to-all-done.1 = f32[64,1,2048]{2,1,0:T(1,128)} async-done(((f32[64,1,2048]{2,1,0:T(1,128)}), f32[64,1,2048]{2,1,0:T(1,128)}, u32[]{:S(2)}, u32[]{:S(2)}) %all-to-all-start.1) | async-done | bytes 524320 | tf_op jit(solution)/shard_map/while/body/eval_jaxpr/all_to_all | solution.py:19
  299.6 3.7 reduce.7
  303.3 2.5 reshape.189
  307.2 2.7 fusion.36
  312.1 1.7 fusion.35
  314.9 2.7 reshape.188
  317.6 6.9 %all-to-all-start.1 = ((f32[64,1,2048]{2,1,0:T(1,128)}), f32[64,1,2048]{2,1,0:T(1,128)}, u32[]{:S(2)}, u32[]{:S(2)}) async-start(f32[64,1,2048]{2,1,0:T(1,128)} %reshape.188), calls=%async_computation.1 | async-start | bytes 1048576 | tf_op jit(solution)/shard_map/while/body/eval_jaxpr/all_to_all | solution.py:19
  326.5 29.2 %all-to-all-done.1 = f32[64,1,2048]{2,1,0:T(1,128)} async-done(((f32[64,1,2048]{2,1,0:T(1,128)}), f32[64,1,2048]{2,1,0:T(1,128)}, u32[]{:S(2)}, u32[]{:S(2)}) %all-to-all-start.1) | async-done | bytes 524320 | tf_op jit(solution)/shard_map/while/body/eval_jaxpr/all_to_all | solution.py:19
  356.2 3.7 reduce.7
  359.9 2.5 reshape.189
  363.8 2.7 fusion.36
  369.0 2.5 broadcast_in_dim.96
  371.4 5.9 %all-to-all-start.4 = ((bf16[8,32,8192]{2,1,0:T(8,128)(2,1)}), bf16[8,32,8192]{2,1,0:T(8,128)(2,1)}, u32[]{:S(2)}, u32[]{:S(2)}) async-start(bf16[8,32,8192]{2,1,0:T(8,128)(2,1)} %broadcast_in_dim.96), calls=%async_computation.4 | async-start | bytes 8388608 | tf_op jit(solution)/shard_map/all_to_all | solution.py:19
  378.0 47.6 %all-to-all-done.4 = bf16[8,32,8192]{2,1,0:T(8,128)(2,1)} async-done(((bf16[8,32,8192]{2,1,0:T(8,128)(2,1)}), bf16[8,32,8192]{2,1,0:T(8,128)(2,1)}, u32[]{:S(2)}, u32[]{:S(2)}) %all-to-all-start.4) | async-done | bytes 4194336 | tf_op jit(solution)/shard_map/all_to_all | solution.py:19
  425.6 2.9 convert_reduce_fusion
  429.4 16.9 %psum.30 = f32[128,32]{0,1:T(8,128)S(1)} all-reduce(f32[128,32]{0,1:T(8,128)S(1)} %convolution_bitcast_fusion), channel_id=1, replica_groups=mesh['feat_0'=4,'feat_1'=16,'samp'=8] {'feat_0'}, use_global_device_ids=true, to_apply=%region_13.17 | all-reduce | flops 4096 | bytes 32768 | tf_op jit(solution)/shard_map/psum | solution.py:27
  446.3 53.5 %psum.31 = f32[128,32]{0,1:T(8,128)} all-reduce(f32[128,32]{0,1:T(8,128)S(1)} %psum.30), channel_id=1, replica_groups=mesh['feat_0'=4,'feat_1'=16,'samp'=8] {'feat_1'}, use_global_device_ids=true, to_apply=%region_14.18 | all-reduce | flops 4096 | bytes 32768 | tf_op jit(solution)/shard_map/psum | solution.py:27
  (78 shorter events, 38.6 us)
Async XLA Ops:
  6.8 10.4 %copy-start = (bf16[128,8192]{1,0:T(8,128)(2,1)S(1)}, bf16[128,8192]{1,0:T(8,128)(2,1)}, u32[]{:S(2)}) copy-start(bf16[128,8192]{1,0:T(8,128)(2,1)} %param.14) | copy-start | bytes 6291460
  6.8 52.8 %copy-start.6 = (s32[2,128]{1,0:T(2,128)S(1)}, s32[2,128]{1,0:T(2,128)}, u32[]{:S(2)}) copy-start(s32[2,128]{1,0:T(2,128)} %param.17) | copy-start | bytes 3076
  6.8 58.8 %all-to-all-start.2 = ((bf16[8,32,8192]{2,1,0:T(8,128)(2,1)}), bf16[8,32,8192]{2,1,0:T(8,128)(2,1)}, u32[]{:S(2)}, u32[]{:S(2)}) async-start(bf16[8,32,8192]{2,1,0:T(8,128)(2,1)} %broadcast_in_dim.94), calls=%async_computation.2 | async-start | bytes 8388608 | tf_op jit(solution)/shard_map/all_to_all | solution.py:19
  68.4 1.1 copy-start.1
  77.3 44.9 %all-to-all-start = ((f32[64,1,2048]{2,1,0:T(1,128)}), f32[64,1,2048]{2,1,0:T(1,128)}, u32[]{:S(2)}, u32[]{:S(2)}) async-start(f32[64,1,2048]{2,1,0:T(1,128)} %reshape.176), calls=%async_computation | async-start | bytes 1048576 | tf_op jit(solution)/shard_map/while/body/eval_jaxpr/all_to_all | solution.py:19
  140.7 38.1 %all-to-all-start = ((f32[64,1,2048]{2,1,0:T(1,128)}), f32[64,1,2048]{2,1,0:T(1,128)}, u32[]{:S(2)}, u32[]{:S(2)}) async-start(f32[64,1,2048]{2,1,0:T(1,128)} %reshape.176), calls=%async_computation | async-start | bytes 1048576 | tf_op jit(solution)/shard_map/while/body/eval_jaxpr/all_to_all | solution.py:19
  194.6 6.1 %copy-start.5 = (f32[128,32]{0,1:T(8,128)S(1)}, f32[128,32]{0,1:T(8,128)}, u32[]{:S(2)}) copy-start(f32[128,32]{0,1:T(8,128)} %param.16) | copy-start | bytes 49156
  194.6 54.3 %all-to-all-start.3 = ((bf16[8,32,8192]{2,1,0:T(8,128)(2,1)}), bf16[8,32,8192]{2,1,0:T(8,128)(2,1)}, u32[]{:S(2)}, u32[]{:S(2)}) async-start(bf16[8,32,8192]{2,1,0:T(8,128)(2,1)} %broadcast_in_dim.95), calls=%async_computation.3 | async-start | bytes 8388608 | tf_op jit(solution)/shard_map/all_to_all | solution.py:19
  200.6 51.2 %copy-start.2 = (f32[32,8192]{1,0:T(8,128)S(1)}, f32[32,8192]{1,0:T(8,128)}, u32[]{:S(2)}) copy-start(f32[32,8192]{1,0:T(8,128)} %copy-done.1) | copy-start | bytes 3145732
  252.0 1.1 copy-start.3
  260.9 38.2 %all-to-all-start.1 = ((f32[64,1,2048]{2,1,0:T(1,128)}), f32[64,1,2048]{2,1,0:T(1,128)}, u32[]{:S(2)}, u32[]{:S(2)}) async-start(f32[64,1,2048]{2,1,0:T(1,128)} %reshape.188), calls=%async_computation.1 | async-start | bytes 1048576 | tf_op jit(solution)/shard_map/while/body/eval_jaxpr/all_to_all | solution.py:19
  317.6 38.1 %all-to-all-start.1 = ((f32[64,1,2048]{2,1,0:T(1,128)}), f32[64,1,2048]{2,1,0:T(1,128)}, u32[]{:S(2)}, u32[]{:S(2)}) async-start(f32[64,1,2048]{2,1,0:T(1,128)} %reshape.188), calls=%async_computation.1 | async-start | bytes 1048576 | tf_op jit(solution)/shard_map/while/body/eval_jaxpr/all_to_all | solution.py:19
  371.4 54.2 %all-to-all-start.4 = ((bf16[8,32,8192]{2,1,0:T(8,128)(2,1)}), bf16[8,32,8192]{2,1,0:T(8,128)(2,1)}, u32[]{:S(2)}, u32[]{:S(2)}) async-start(bf16[8,32,8192]{2,1,0:T(8,128)(2,1)} %broadcast_in_dim.96), calls=%async_computation.4 | async-start | bytes 8388608 | tf_op jit(solution)/shard_map/all_to_all | solution.py:19
  377.3 51.2 %copy-start.4 = (f32[32,8192]{1,0:T(8,128)S(1)}, f32[32,8192]{1,0:T(8,128)}, u32[]{:S(2)}) copy-start(f32[32,8192]{1,0:T(8,128)} %copy-done.3) | copy-start | bytes 3145732
where the time goes:
time: 502 us; the launch traced here: 500 us
  waiting for transfers between devices  219 us (44%)
  blocking collectives  112 us (22%)
  starting transfers between devices  56.7 us (11%)
  local copies, waits for them, and re-layouts  53.6 us (11%)
  other arithmetic  37.3 us (7%)
  matrix products  20.4 us (4%)
    all_to_all x7, waiting for transfers between devices, from_everyone(): lax.all_to_all(jnp.broadcast_to(x[None], (size, *x.shape)), axis, 0, 0, t...  219 us
    psum x4, blocking collectives, over_axes(): return functools.reduce(lax.psum, axes, x)  112 us
    all_to_all x7, starting transfers between devices, from_everyone(): lax.all_to_all(jnp.broadcast_to(x[None], (size, *x.shape)), axis, 0, 0, t...  56.7 us
    while x12, local copies, waits for them, and re-layouts  25.1 us
    all_to_all x4, other arithmetic, from_everyone(): lax.all_to_all(jnp.broadcast_to(x[None], (size, *x.shape)), axis, 0, 0, t...  14.9 us
    dot_general x5, matrix products, contract_rows(): lax.dot_general(left_side, right_side, (((0,), (0,)), ((), ())), preferre...  12.8 us
  transfers between devices with their start and end apart: 7, of which 7 were waited for; matrix products, arithmetic and copies ran while one was open for 2% of the time, Pallas kernels for 0%

commit v1 on v0

v1 whole, which is shorter than its diff:
```python
import functools

import jax
import jax.numpy as jnp
from jax import lax
from jax.experimental import pallas as pl
from jax.experimental.pallas import tpu as pltpu
from jax.sharding import Mesh
from jax.sharding import PartitionSpec as P

BLOCK = 64
ROUNDS = 2
GRID = (4, 16, 4, 2)
NAMES = ("y", "z", "x", "c")
MESH = pl.DeviceIdType.MESH
FEAT = ("y", "z")
SAMP = ("x", "c")

reg_scale = 0.9


def mm(left, right):
    return lax.dot_general(left, right, (((1,), (0,)), ((), ())), preferred_element_type=jnp.float32)


def mm_t(left, right):
    return lax.dot_general(left, right, (((1,), (1,)), ((), ())), preferred_element_type=jnp.float32)


def kernel(
    sizes,
    lam_total,
    feat_hbm,
    labels_ref,
    alpha_ref,
    order_ref,
    alpha_out,
    scores_out,
    own,
    turned,
    coef,
    wacc,
    part_m,
    got_m,
    got_z,
    signs_s,
    alpha_s,
    last,
    gram_p,
    gram_y,
    gram_z,
    gram,
    loc_sem,
    turn_send,
    turn_recv,
    coef_send,
    coef_recv,
    m_send,
    m_recv,
    z_send,
    z_recv,
    g_send,
    g_recv,
    last_send,
    last_recv,
):
    ny, nz, nx, nc = sizes
    y, z, x, c = (lax.axis_index(name) for name in NAMES)
    ns = nx * nc
    samp = x * nc + c
    rows, cols = feat_hbm.shape
    lab = labels_ref.shape[1]
    lp = lab // ny
    gp = rows // ny
    share = cols // ns
    pieces = ny * ns
    me = y * ns + samp

    def samp_dev(peer):
        return (y, z, peer // nc, peer % nc)

    def plane_dev(peer):
        peer_s = peer % ns
        return (peer // ns, z, peer_s // nc, peer_s % nc)

    def z_dev(peer):
        return (y, peer, x, c)

    def y_dev(peer):
        return (peer, z, x, c)

    def others(count, index, body):
        def step(i, carry):
            body(lax.rem(index + i, count))
            return carry

        lax.fori_loop(1, count, step, 0)

    def send(src, dst, s_sem, r_sem, dev):
        pltpu.make_async_remote_copy(
            src_ref=src, dst_ref=dst, send_sem=s_sem, recv_sem=r_sem, device_id=dev, device_id_type=MESH
        ).start()

    def wait_bytes(ref, sem):
        pltpu.make_async_copy(ref, ref, sem).wait()

    def tile(ref, peer_s, peer_y):
        return ref.at[pl.ds(pl.multiple_of(peer_y * lp, lp), lp), pl.ds(pl.multiple_of(peer_s * rows, rows), rows)]

    barrier = pltpu.get_barrier_semaphore()

    def hello(dev):
        pl.semaphore_signal(barrier, inc=1, device_id=dev, device_id_type=MESH)

    others(pieces, me, lambda p: hello(plane_dev(p)))
    others(nz, z, lambda p: hello(z_dev(p)))

    load_own = pltpu.make_async_copy(feat_hbm, own, loc_sem.at[0])
    load_own.start()
    my_rows = pl.ds(pl.multiple_of(samp * rows, rows), rows)
    load_turn = pltpu.make_async_copy(
        feat_hbm.at[:, pl.ds(pl.multiple_of(samp * share, share), share)], turned.at[my_rows], loc_sem.at[1]
    )
    load_turn.start()

    signs_s[...] = labels_ref[...].astype(jnp.float32).T
    alpha_s[...] = alpha_ref[...].T
    coef[0, :, my_rows] = (alpha_s[...] * signs_s[...]).astype(jnp.bfloat16).astype(jnp.float32)

    pl.semaphore_wait(barrier, pieces - 1 + nz - 1)

    others(
        ns,
        samp,
        lambda p: send(
            coef.at[0, :, my_rows], coef.at[0, :, my_rows], coef_send.at[0], coef_recv.at[0], samp_dev(p)
        ),
    )
    others(
        ns,
        samp,
        lambda p: send(
            feat_hbm.at[:, pl.ds(pl.multiple_of(p * share, share), share)],
            turned.at[my_rows],
            turn_send,
            turn_recv,
            samp_dev(p),
        ),
    )

    load_own.wait()
    gram_p[...] = mm_t(own[...], own[...])

    def gpiece(ref, peer_y):
        return ref.at[pl.ds(pl.multiple_of(peer_y * gp, gp), gp)]

    others(ny, y, lambda p: send(gpiece(gram_p, p), gram_y.at[y], g_send.at[0], g_recv.at[0], y_dev(p)))
    gram_y[y] = gpiece(gram_p, y)[...]
    if ny > 1:
        wait_bytes(gram_y.at[pl.ds(0, ny - 1)], g_recv.at[0])
    gram_z[z] = jnp.sum(gram_y[...], axis=0)
    others(nz, z, lambda p: send(gram_z.at[z], gram_z.at[z], g_send.at[1], g_recv.at[1], z_dev(p)))
    wait_bytes(gram_z.at[pl.ds(0, nz - 1)], g_recv.at[1])
    gpiece(gram, y)[...] = jnp.sum(gram_z[...], axis=0)
    others(ny, y, lambda p: send(gpiece(gram, y), gpiece(gram, y), g_send.at[2], g_recv.at[2], y_dev(p)))
    if ny > 1:
        wait_bytes(gram.at[pl.ds(0, rows - gp)], g_recv.at[2])

    g_all = gram[...]
    g_high = g_all.astype(jnp.bfloat16)
    g_low = (g_all - g_high.astype(jnp.float32)).astype(jnp.bfloat16)
    row_i = lax.broadcasted_iota(jnp.int32, (rows, rows), 0)
    col_i = lax.broadcasted_iota(jnp.int32, (rows, rows), 1)
    norms = 1.0 + jnp.sum(jnp.where(row_i == col_i, g_all, 0.0), axis=0, keepdims=True)
    early = (lax.broadcasted_iota(jnp.int32, (8, rows), 1) < BLOCK).astype(jnp.bfloat16)
    firsts = []
    for r in range(ROUNDS):
        hot = (row_i == order_ref[r : r + 1, :]).astype(jnp.bfloat16)
        firsts.append(mm_t(early, hot)[0:1] > 0.5)

    my_labels = pl.ds(pl.multiple_of(y * lp, lp), lp)
    sign = signs_s[my_labels, :]
    alpha = alpha_s[my_labels, :]

    load_turn.wait()
    wait_bytes(coef.at[0, :, pl.ds(0, (ns - 1) * rows)], coef_recv.at[0])
    wait_bytes(turned.at[pl.ds(0, (ns - 1) * rows)], turn_recv)

    for r in range(ROUNDS + 1):
        step = mm(coef[r].astype(jnp.bfloat16), turned[...])
        wacc[...] = step if r == 0 else wacc[...] + step * (1.0 / ns)
        part_m[r] = mm_t((wacc[...] * (1.0 / lam_total)).astype(jnp.bfloat16), turned[...])
        got_m[r, me] = tile(part_m.at[r], samp, y)[...]
        others(
            pieces,
            me,
            lambda p: send(tile(part_m.at[r], p % ns, p // ns), got_m.at[r, me], m_send.at[r], m_recv.at[r], plane_dev(p)),
        )
        wait_bytes(got_m.at[r, pl.ds(0, pieces - 1)], m_recv.at[r])
        got_z[r, z] = jnp.sum(got_m[r], axis=0)
        others(nz, z, lambda p: send(got_z.at[r, z], got_z.at[r, z], z_send.at[r], z_recv.at[r], z_dev(p)))
        wait_bytes(got_z.at[r, pl.ds(0, nz - 1)], z_recv.at[r])
        margins = jnp.sum(got_z[r], axis=0)
        if r == ROUNDS:
            break
        first = firsts[r]
        up_0 = jnp.clip(alpha + lam_total * (1.0 - sign * margins) / norms, 0.0, 1.0)
        ch_0 = jnp.where(first, (up_0 - alpha) * sign, 0.0).astype(jnp.bfloat16)
        moved = mm(ch_0, g_high) + mm(ch_0, g_low)
        margins = margins + moved * (1.0 / lam_total)
        up_1 = jnp.clip(alpha + lam_total * (1.0 - sign * margins) / norms, 0.0, 1.0)
        ch_1 = ((up_1 - alpha) * sign).astype(jnp.bfloat16)
        change = jnp.where(first, ch_0.astype(jnp.float32), ch_1.astype(jnp.float32))
        alpha = alpha + (jnp.where(first, up_0, up_1) - alpha) * (1.0 / ns)
        spot = tile(coef.at[r + 1], samp, y)
        spot[...] = change
        others(
            pieces,
            me,
            lambda p: send(spot, spot, coef_send.at[r + 1], coef_recv.at[r + 1], plane_dev(p)),
        )
        if r == ROUNDS - 1:
            last[0, my_labels] = alpha
            others(
                ny,
                y,
                lambda p: send(last.at[0, my_labels], last.at[0, my_labels], last_send.at[0], last_recv.at[0], y_dev(p)),
            )
        wait_bytes(got_m.at[r + 1, pl.ds(0, pieces - 1)], coef_recv.at[r + 1])

    last[1, my_labels] = margins
    others(
        ny, y, lambda p: send(last.at[1, my_labels], last.at[1, my_labels], last_send.at[1], last_recv.at[1], y_dev(p))
    )
    if ny > 1:
        wait_bytes(last.at[0, pl.ds(0, lab - lp)], last_recv.at[0])
    alpha_out[...] = last[0].T
    if ny > 1:
        wait_bytes(last.at[1, pl.ds(0, lab - lp)], last_recv.at[1])
    scores_out[...] = last[1].T

    wait_bytes(turned.at[pl.ds(0, (ns - 1) * rows)], turn_send)
    wait_bytes(coef.at[0, :, pl.ds(0, (ns - 1) * rows)], coef_send.at[0])
    for r in range(ROUNDS + 1):
        wait_bytes(got_m.at[r, pl.ds(0, pieces - 1)], m_send.at[r])
        wait_bytes(got_z.at[r, pl.ds(0, nz - 1)], z_send.at[r])
        if r:
            wait_bytes(got_m.at[r, pl.ds(0, pieces - 1)], coef_send.at[r])
    wait_bytes(gram_z.at[pl.ds(0, nz - 1)], g_send.at[1])
    if ny > 1:
        wait_bytes(gram_y.at[pl.ds(0, ny - 1)], g_send.at[0])
        wait_bytes(gram_y.at[pl.ds(0, ny - 1)], g_send.at[2])
        for i in range(2):
            wait_bytes(last.at[i, pl.ds(0, lab - lp)], last_send.at[i])


def per_device(sizes, features, labels, alpha_start, order):
    ny, nz, nx, nc = sizes
    ns = nx * nc
    rows, cols = features.shape
    lab = labels.shape[1]
    lp, gp, share = lab // ny, rows // ny, cols // ns
    lam_total = reg_scale * cols * ny * nz
    n = ROUNDS + 1
    f32 = jnp.float32
    vmem = pl.BlockSpec(memory_space=pltpu.VMEM)
    dma = pltpu.SemaphoreType.DMA
    return pl.pallas_call(
        functools.partial(kernel, sizes, lam_total),
        out_shape=(jax.ShapeDtypeStruct((rows, lab), f32),) * 2,
        in_specs=[pl.BlockSpec(memory_space=pl.ANY), vmem, vmem, vmem],
        out_specs=(vmem, vmem),
        scratch_shapes=[
            pltpu.VMEM((rows, cols), jnp.bfloat16),
            pltpu.VMEM((ns * rows, share), jnp.bfloat16),
            pltpu.VMEM((n, lab, ns * rows), f32),
            pltpu.VMEM((lab, share), f32),
            pltpu.VMEM((n, lab, ns * rows), f32),
            pltpu.VMEM((n, ny * ns, lp, rows), f32),
            pltpu.VMEM((n, nz, lp, rows), f32),
            pltpu.VMEM((lab, rows), f32),
            pltpu.VMEM((lab, rows), f32),
            pltpu.VMEM((2, lab, rows), f32),
            pltpu.VMEM((rows, rows), f32),
            pltpu.VMEM((ny, gp, rows), f32),
            pltpu.VMEM((nz, gp, rows), f32),
            pltpu.VMEM((rows, rows), f32),
            dma((2,)),
            dma(()),
            dma(()),
            dma((n,)),
            dma((n,)),
            dma((n,)),
            dma((n,)),
            dma((n,)),
            dma((n,)),
            dma((3,)),
            dma((3,)),
            dma((2,)),
            dma((2,)),
        ],
        compiler_params=pltpu.CompilerParams(
            collective_id=0, has_side_effects=True, vmem_limit_bytes=48 * 1024 * 1024
        ),
        name="dual_rounds",
    )(features, labels, alpha_start, order)


def solution(mesh, grid=GRID):
    finer = Mesh(mesh.devices.reshape(grid), NAMES)
    placed = (P(SAMP, FEAT), P(SAMP, None), P(SAMP, None), P(None, SAMP))
    return jax.shard_map(
        functools.partial(per_device, grid),
        mesh=finer,
        in_specs=placed,
        out_specs=(P(SAMP, None), P(SAMP, None)),
        check_vma=False,
    )
```

time: 502 us -> 108 us (0.22)
  the two profiles are of different devices: /device:TPU:2 before, /device:TPU:1 now
where the time goes in v1:
time: 108 us
  Pallas kernels  102 us (94%)
  local copies, waits for them, and re-layouts  5.26 us (5%)
    pallas_call x1, Pallas kernels, per_device(): pl.pallas_call(functools.partial(kernel, sizes, lam_total), out_shape=(ja...  102 us
    unnamed x6, local copies, waits for them, and re-layouts  3.9 us

profile of v1, /device:TPU:1, one launch (start us, length us, event | category | flops | bytes accessed | tf_op | source)
XLA Modules:
  0.0 107.9 jit_solution(10548587918938002930)
XLA Ops:
  0.6 0.8 copy.6.labels_ref
  1.4 0.8 copy.7.alpha_ref
  2.3 0.0 copy-start
  2.3 1.6 %copy-done = bf16[128,8192]{1,0:T(8,128)(2,1)S(1)} copy-done((bf16[128,8192]{1,0:T(8,128)(2,1)S(1)}, bf16[128,8192]{1,0:T(8,128)(2,1)}, u32[]{:S(2)}) %copy-start) | copy-done | bytes 2097176
  3.9 0.0 copy-start.1
  3.9 0.7 copy-done.1
  4.5 102.0 %dual_rounds.1 = (f32[128,32]{1,0:T(8,128)S(1)}, f32[128,32]{1,0:T(8,128)S(1)}) custom-call(bf16[128,8192]{1,0:T(8,128)(2,1)S(1)} %copy-done, s32[128,32]{1,0:T(8,128)S(1)} %copy.6.labels_ref, f32[128,32]{1,0:T(8,128)S(1)} %copy.7.alpha_ref, s32[2,128]{1,0:T(2,128)S(1)} %copy-done.1), custom_call_target="tpu_custom_call" | custom-call | tf_op jit(solution)/shard_map/dual_rounds/pallas_call | solution.py:268
  106.5 0.7 copy.8
  107.2 0.7 copy.9
Async XLA Ops:
  2.3 1.6 %copy-start = (bf16[128,8192]{1,0:T(8,128)(2,1)S(1)}, bf16[128,8192]{1,0:T(8,128)(2,1)}, u32[]{:S(2)}) copy-start(bf16[128,8192]{1,0:T(8,128)(2,1)} %feat_hbm.1) | copy-start | bytes 6291460
  3.9 0.7 copy-start.1
